TPU v7x, 32 devices: a whole 2x2x4 slice. The times are simulated.
32 devices in a mesh: layer: 2 (over core), px: 4 (over z), py: 4 (over y, x).
Axes of the slice: x: 2, y: 2, z: 4, core: 2. Of those that a mesh axis runs over, the one named last changes fastest.
Arguments:
- right_side: float32 [8, 512, 4096], P('layer', 'px', 'py'), may hold values from -30 to 30
- row_conduct: float32 [8, 512, 4096], P('layer', 'px', 'py'), may hold values from 0.5 to 2
- column_conduct: float32 [8, 512, 4096], P('layer', 'px', 'py'), may hold values from 0.5 to 2
- via_conduct: float32 [8, 512, 4096], P('layer', 'px', 'py'), may hold values from 0.5 to 4
- via_mask: int32 [8, 512, 4096], P('layer', 'px', 'py'), may hold values 0 or 1
- ground_conduct: float32 [8, 512, 4096], P('layer', 'px', 'py'), may hold values from 0.01 to 0.1
Outputs:
- solution_field: float32 [8, 512, 4096], P('layer', 'px', 'py')
- residual: float32 [8, 512, 4096], P('layer', 'px', 'py')
All inputs are finite; a program needn't handle non-finite values. No bound on the sum of `via_mask` on one device may be relied on, other than what follows from the above.
Results may differ from a plain program's by a relative error of at most 0.0001.
Values sent between devices are 32-bit elements; how exact they have to be, the bound alone decides.
A program may use at most 128 MiB of HBM per device.

v0:
```python
import jax
import jax.numpy as jnp
from jax import lax
from jax.sharding import PartitionSpec as P

ITERS = 2


def extended(value, sides, width):
    for axis, dim in sides:
        count, length = (lax.axis_size(axis), value.shape[dim])
        up = [(i, (i + 1) % count) for i in range(count - 1)]
        down = [(j, i) for i, j in up]
        last = lax.slice_in_dim(value, length - width, length, axis=dim)
        initial = lax.slice_in_dim(value, 0, width, axis=dim)
        before = lax.ppermute(last, axis, up)
        after = lax.ppermute(initial, axis, down)
        value = jnp.concatenate([before, value, after], axis=dim)
    return value


def from_behind(value, axis, by):
    count = lax.axis_size(axis)
    pairs = [(i, i + by) for i in range(count) if 0 <= i + by < count]
    return lax.ppermute(value, axis, pairs)


def factor_layers(diagonal, vertical, vertical_below, carried):
    gains = []
    inverses = []
    previous = carried
    for index in range(diagonal.shape[0]):
        inverse = 1.0 / (diagonal[index] - vertical_below[index] * previous)
        previous = vertical[index] * inverse
        gains.append(previous)
        inverses.append(inverse)
    return (jnp.stack(gains), jnp.stack(inverses))


def forward_layers(residual, vertical_below, inverses, carried):
    values = []
    previous = carried
    for index in range(residual.shape[0]):
        previous = (residual[index] + vertical_below[index] * previous) * inverses[index]
        values.append(previous)
    return jnp.stack(values)


def back_layers(forward, gains, carried):
    count = forward.shape[0]
    values = [None] * count
    following = carried
    for index in range(count - 1, -1, -1):
        following = forward[index] + gains[index] * following
        values[index] = following
    return jnp.stack(values)


def operate(field, coeffs):
    diagonal, row_conduct, row_upper, column_conduct, column_left, vertical, vertical_below = coeffs
    padded = extended(field, (("layer", 0), ("px", 1), ("py", 2)), 1)
    return (
        diagonal * field
        - row_conduct * padded[1:-1, 2:, 1:-1]
        - row_upper * padded[1:-1, :-2, 1:-1]
        - column_conduct * padded[1:-1, 1:-1, 2:]
        - column_left * padded[1:-1, 1:-1, :-2]
        - vertical * padded[2:, 1:-1, 1:-1]
        - vertical_below * padded[:-2, 1:-1, 1:-1]
    )


def paired_sums(residual, precond, image):
    return lax.psum((jnp.sum(residual * precond), jnp.sum(image * precond)), ("layer", "px", "py"))


def shards(right_side, row_conduct, column_conduct, via_conduct, via_mask, ground_conduct):
    depth = right_side.shape[0]
    members = lax.axis_size("layer")
    layers_total = depth * members
    level = lax.axis_index("layer") * depth + jnp.arange(depth, dtype=jnp.int32)
    keep = (level < layers_total - 1).astype(jnp.float32)[:, None, None]
    vertical = via_conduct * via_mask.astype(jnp.float32) * keep
    row_edge = from_behind(row_conduct[:, -1:, :], "px", 1)
    row_upper = jnp.concatenate([row_edge, row_conduct[:, :-1, :]], axis=1)
    column_edge = from_behind(column_conduct[:, :, -1:], "py", 1)
    column_left = jnp.concatenate([column_edge, column_conduct[:, :, :-1]], axis=2)
    vertical_edge = from_behind(vertical[-1:], "layer", 1)
    vertical_below = jnp.concatenate([vertical_edge, vertical[:-1]], axis=0)
    diagonal = (
        ground_conduct
        + row_conduct
        + row_upper
        + column_conduct
        + column_left
        + vertical
        + vertical_below
    )
    coeffs = (
        diagonal,
        row_conduct,
        row_upper,
        column_conduct,
        column_left,
        vertical,
        vertical_below,
    )
    plane = jnp.zeros_like(right_side[0])
    carried = plane
    gains, inverses = factor_layers(diagonal, vertical, vertical_below, carried)
    carried = from_behind(gains[-1], "layer", 1)
    gains, inverses = factor_layers(diagonal, vertical, vertical_below, carried)

    def precondition(residual):
        incoming = plane
        forward = forward_layers(residual, vertical_below, inverses, incoming)
        incoming = from_behind(forward[-1], "layer", 1)
        forward = forward_layers(residual, vertical_below, inverses, incoming)
        returning = plane
        solved = back_layers(forward, gains, returning)
        returning = from_behind(solved[0], "layer", -1)
        return back_layers(forward, gains, returning)

    solution_field = jnp.zeros_like(right_side)
    residual = right_side
    precond = precondition(residual)
    image = operate(precond, coeffs)
    rho, curvature = paired_sums(residual, precond, image)
    alpha = rho / curvature
    direction, along = (precond, image)
    for step in range(ITERS):
        solution_field = solution_field + alpha * direction
        residual = residual - alpha * along
        if step + 1 < ITERS:
            precond = precondition(residual)
            image = operate(precond, coeffs)
            rho_next, curvature = paired_sums(residual, precond, image)
            ratio = rho_next / rho
            alpha = rho_next / (curvature - ratio * rho_next / alpha)
            direction = precond + ratio * direction
            along = image + ratio * along
            rho = rho_next
    return (solution_field, residual)


def solution(mesh):
    in_specs = (
        P("layer", "px", "py"),
        P("layer", "px", "py"),
        P("layer", "px", "py"),
        P("layer", "px", "py"),
        P("layer", "px", "py"),
        P("layer", "px", "py"),
    )
    out_specs = (P("layer", "px", "py"), P("layer", "px", "py"))
    return jax.shard_map(shards, mesh=mesh, in_specs=in_specs, out_specs=out_specs, check_vma=False)
```

profile of v0, /device:TPU:0, one launch (start us, length us, event | category | flops | bytes accessed | tf_op | source)
XLA Modules:
  0.0 236.2 jit_solution(5052994226875419765)
XLA Ops:
  0.7 3.1 %multiply_multiply_fusion = f32[4,128,1024]{2,1,0:T(8,128)S(1)} fusion(f32[4,128,1024]{2,1,0:T(8,128)} %param.9, s32[4,128,1024]{2,1,0:T(8,128)} %param.10, f32[4]{0:T(128)S(1)} %compare_convert_fusion), kind=kLoop, calls=%fused_computation.53 | loop fusion | flops 1572864 | bytes 6291472 | tf_op jit(solution)/shard_map/mul | solution.py:83
  3.8 2.6 %collective-permute-start = (f32[1,128,1024]{2,1,0:T(8,128)S(1)}, f32[1,128,1024]{2,1,0:T(8,128)S(1)}, u32[]{:S(2)}, u32[]{:S(2)}) collective-permute-start(f32[1,128,1024]{2,1,0:T(8,128)S(1)} %slice.202), channel_id=1, source_target_pairs={{0,16},{1,17},{2,18},{3,19},{4,20},{5,21},{6,22},{7,23},{8,24},{9,... | collective-permute-start | bytes 1572872 | tf_op jit(solution)/shard_map/ppermute | solution.py:25
  6.4 4.3 %collective-permute-start.1 = (f32[4,1,1024]{2,1,0:T(1,128)S(1)}, f32[4,1,1024]{2,1,0:T(1,128)S(1)}, u32[]{:S(2)}, u32[]{:S(2)}) collective-permute-start(f32[4,1,1024]{2,1,0:T(1,128)S(1)} %slice.173), channel_id=1, source_target_pairs={{0,4},{4,8},{8,12},{1,5},{5,9},{9,13},{2,6},{6,10},{10,14},{3,7},{... | collective-permute-start | bytes 49160 | tf_op jit(solution)/shard_map/ppermute | solution.py:25
  10.9 3.4 %collective-permute-start.2 = (f32[4,128,1]{2,1,0:T(8,128)S(1)}, f32[4,128,1]{2,1,0:T(8,128)S(1)}, u32[]{:S(2)}, u32[]{:S(2)}) collective-permute-start(f32[4,128,1]{2,1,0:T(8,128)S(1)} %slice.175), channel_id=1, source_target_pairs={{0,1},{1,2},{2,3},{4,5},{5,6},{6,7},{8,9},{9,10},{10,11},{12,13},{... | collective-permute-start | bytes 6152 | tf_op jit(solution)/shard_map/ppermute | solution.py:25
  14.4 4.7 %collective-permute-done.2 = f32[4,128,1]{2,1,0:T(8,128)S(1)} collective-permute-done((f32[4,128,1]{2,1,0:T(8,128)S(1)}, f32[4,128,1]{2,1,0:T(8,128)S(1)}, u32[]{:S(2)}, u32[]{:S(2)}) %collective-permute-start.2) | collective-permute-done | bytes 2080 | tf_op jit(solution)/shard_map/ppermute | solution.py:25
  19.1 1.8 add_add_fusion
  21.3 1.5 collective-permute-start.3
  22.8 1.5 collective-permute-done.3
  24.3 0.9 fusion.33
  25.2 2.3 collective-permute-start.4
  27.5 1.5 collective-permute-done.4
  29.0 1.0 multiply_add_fusion.8
  30.1 1.3 collective-permute-start.5
  31.4 2.5 %collective-permute-done.5 = f32[128,1024]{1,0:T(8,128)S(1)} collective-permute-done((f32[128,1024]{1,0:T(8,128)S(1)}, f32[128,1024]{1,0:T(8,128)S(1)}, u32[]{:S(2)}, u32[]{:S(2)}) %collective-permute-start.5) | collective-permute-done | bytes 524320 | tf_op jit(solution)/shard_map/ppermute | solution.py:25
  34.2 2.1 collective-permute-start.6
  36.2 1.5 collective-permute-done.6
  37.8 0.7 copy-done.32
  39.0 1.3 collective-permute-start.7
  40.5 2.4 collective-permute-done.7
  42.9 3.6 %collective-permute-start.9 = (f32[6,1,1024]{2,1,0:T(1,128)S(1)}, f32[6,1,1024]{2,1,0:T(1,128)S(1)}, u32[]{:S(2)}, u32[]{:S(2)}) collective-permute-start(f32[6,1,1024]{2,1,0:T(1,128)S(1)} %get-tuple-element.42), channel_id=1, source_target_pairs={{0,4},{4,8},{8,12},{1,5},{5,9},{9,13},{2,6},{6,10},{10,14},{3,7},{... | collective-permute-start | bytes 73736 | tf_op jit(solution)/shard_map/ppermute | solution.py:16
  46.6 1.3 collective-permute-start.8
  48.1 4.2 %collective-permute-done.8 = f32[6,1,1024]{2,1,0:T(1,128)S(1)} collective-permute-done((f32[6,1,1024]{2,1,0:T(1,128)S(1)}, f32[6,1,1024]{2,1,0:T(1,128)S(1)}, u32[]{:S(2)}, u32[]{:S(2)}) %collective-permute-start.8) | collective-permute-done | bytes 24608 | tf_op jit(solution)/shard_map/ppermute | solution.py:17
  52.5 1.3 collective-permute-start.10
  53.8 5.0 %collective-permute-start.11 = (f32[6,130,1]{2,1,0:T(8,128)S(1)}, f32[6,130,1]{2,1,0:T(8,128)S(1)}, u32[]{:S(2)}, u32[]{:S(2)}) collective-permute-start(f32[6,130,1]{2,1,0:T(8,128)S(1)} %get-tuple-element.39), channel_id=1, source_target_pairs={{0,1},{1,2},{2,3},{4,5},{5,6},{6,7},{8,9},{9,10},{10,11},{12,13},{... | collective-permute-start | bytes 9368 | tf_op jit(solution)/shard_map/ppermute | solution.py:16
  58.8 8.5 %collective-permute-done.10 = f32[6,130,1]{2,1,0:T(8,128)S(1)} collective-permute-done((f32[6,130,1]{2,1,0:T(8,128)S(1)}, f32[6,130,1]{2,1,0:T(8,128)S(1)}, u32[]{:S(2)}, u32[]{:S(2)}) %collective-permute-start.10) | collective-permute-done | bytes 3152 | tf_op jit(solution)/shard_map/ppermute | solution.py:17
  67.4 9.0 %multiply_reduce_fusion.2 = (f32[]{:T(128)}, f32[]{:T(128)}, f32[4,128,1024]{2,1,0:T(8,128)}) fusion(f32[1,128,1024]{2,1,0:T(8,128)S(1)} %bitcast.234, f32[1,128,1024]{2,1,0:T(8,128)S(1)} %bitcast.241, f32[1,128,1024]{2,1,0:T(8,128)S(1)} %bitcast.239, f32[1,128,1024]{2,1,0:T(8,128)S(1)} %get-tuple-element.21, f32[4,128,1024]{2,1,0:T(8,128)S(1)} %copy-done.5, ...), kind=kLoop, calls=%fused_computation.50 | loop fusion | flops 22544384 | bytes 25221224 | tf_op jit(solution)/shard_map/reduce_sum | solution.py:74
  76.5 47.6 %all-reduce.1 = (f32[]{:T(128)}, f32[]{:T(128)}) all-reduce(f32[]{:T(128)} %get-tuple-element.5, f32[]{:T(128)} %get-tuple-element.4), channel_id=1, replica_groups=mesh['layer'=2,'px'=4,'py'=4] {'layer','px','py'}, use_global_device_ids=true, to_apply=%region_1.0 | all-reduce | flops 2 | bytes 16 | tf_op jit(solution)/shard_map/psum | solution.py:74
  125.4 2.8 %multiply_subtract_fusion.1 = f32[4,128,1024]{2,1,0:T(8,128)S(1)} fusion(f32[4,128,1024]{2,1,0:T(8,128)} %param.6, f32[4,128,1024]{2,1,0:T(8,128)} %get-tuple-element.19, f32[]{:T(128)S(6)} %div.44), kind=kLoop, calls=%fused_computation.49 | loop fusion | flops 1048576 | bytes 6291460 | tf_op jit(solution)/shard_map/sub | solution.py:133
  128.2 0.7 add_multiply_fusion.3
  128.9 1.6 collective-permute-start.12
  130.6 1.3 collective-permute-done.12
  131.9 1.0 multiply_add_fusion.4
  132.9 1.3 collective-permute-start.13
  134.2 2.5 %collective-permute-done.13 = f32[128,1024]{1,0:T(8,128)S(1)} collective-permute-done((f32[128,1024]{1,0:T(8,128)S(1)}, f32[128,1024]{1,0:T(8,128)S(1)}, u32[]{:S(2)}, u32[]{:S(2)}) %collective-permute-start.13) | collective-permute-done | bytes 524320 | tf_op jit(solution)/shard_map/ppermute | solution.py:25
  137.0 2.1 collective-permute-start.14
  139.1 1.5 collective-permute-done.14
  140.6 0.5 constant_dynamic-update-slice_fusion.10
  141.4 1.3 collective-permute-start.15
  142.9 2.3 collective-permute-done.15
  145.3 2.6 %collective-permute-start.17 = (f32[6,1,1024]{2,1,0:T(1,128)S(1)}, f32[6,1,1024]{2,1,0:T(1,128)S(1)}, u32[]{:S(2)}, u32[]{:S(2)}) collective-permute-start(f32[6,1,1024]{2,1,0:T(1,128)S(1)} %get-tuple-element.40), channel_id=1, source_target_pairs={{0,4},{4,8},{8,12},{1,5},{5,9},{9,13},{2,6},{6,10},{10,14},{3,7},{... | collective-permute-start | bytes 73736 | tf_op jit(solution)/shard_map/ppermute | solution.py:16
  147.9 1.3 collective-permute-start.16
  149.4 4.2 %collective-permute-done.16 = f32[6,1,1024]{2,1,0:T(1,128)S(1)} collective-permute-done((f32[6,1,1024]{2,1,0:T(1,128)S(1)}, f32[6,1,1024]{2,1,0:T(1,128)S(1)}, u32[]{:S(2)}, u32[]{:S(2)}) %collective-permute-start.16) | collective-permute-done | bytes 24608 | tf_op jit(solution)/shard_map/ppermute | solution.py:17
  153.9 1.3 collective-permute-start.18
  155.2 4.8 %collective-permute-start.19 = (f32[6,130,1]{2,1,0:T(8,128)S(1)}, f32[6,130,1]{2,1,0:T(8,128)S(1)}, u32[]{:S(2)}, u32[]{:S(2)}) collective-permute-start(f32[6,130,1]{2,1,0:T(8,128)S(1)} %get-tuple-element.37), channel_id=1, source_target_pairs={{0,1},{1,2},{2,3},{4,5},{5,6},{6,7},{8,9},{9,10},{10,11},{12,13},{... | collective-permute-start | bytes 9368 | tf_op jit(solution)/shard_map/ppermute | solution.py:16
  160.0 8.5 %collective-permute-done.18 = f32[6,130,1]{2,1,0:T(8,128)S(1)} collective-permute-done((f32[6,130,1]{2,1,0:T(8,128)S(1)}, f32[6,130,1]{2,1,0:T(8,128)S(1)}, u32[]{:S(2)}, u32[]{:S(2)}) %collective-permute-start.18) | collective-permute-done | bytes 3152 | tf_op jit(solution)/shard_map/ppermute | solution.py:17
  168.6 10.0 %multiply_reduce_fusion = (f32[]{:T(128)}, f32[]{:T(128)}, f32[4,128,1024]{2,1,0:T(8,128)}) fusion(f32[1,128,1024]{2,1,0:T(8,128)S(1)} %bitcast.237, f32[1,128,1024]{2,1,0:T(8,128)S(1)} %bitcast.245, f32[1,128,1024]{2,1,0:T(8,128)S(1)} %bitcast.243, f32[1,128,1024]{2,1,0:T(8,128)S(1)} %get-tuple-element.12, f32[4,128,1024]{2,1,0:T(8,128)S(1)} %multiply_subtract_fusion.1, ...), kind=kLoop, calls=%fused_computation.47 | loop fusion | flops 22544384 | bytes 25221224 | tf_op jit(solution)/shard_map/reduce_sum | solution.py:74
  178.6 46.8 %all-reduce = (f32[]{:T(128)}, f32[]{:T(128)}) all-reduce(f32[]{:T(128)} %get-tuple-element.3, f32[]{:T(128)} %get-tuple-element.2), channel_id=1, replica_groups=mesh['layer'=2,'px'=4,'py'=4] {'layer','px','py'}, use_global_device_ids=true, to_apply=%region_5.0 | all-reduce | flops 2 | bytes 16 | tf_op jit(solution)/shard_map/psum | solution.py:74
  230.2 5.9 %multiply_subtract_fusion = (f32[4,128,1024]{2,1,0:T(8,128)}, f32[4,128,1024]{2,1,0:T(8,128)}) fusion(f32[4,128,1024]{2,1,0:T(8,128)} %copy-done.4, f32[4,128,1024]{2,1,0:T(8,128)} %get-tuple-element.10, f32[4,128,1024]{2,1,0:T(8,128)} %get-tuple-element.19, f32[]{:T(128)S(6)} %div.45, f32[]{:T(128)S(6)} %div.47, f32[1,128,1024]{2,1,0:T(8,128)} %bitcast.238, ...), kind=kLoop, calls=%fused_computation.45 | loop fusion | flops 7864320 | bytes 14680076 | tf_op jit(solution)/shard_map/sub | solution.py:133
  (96 shorter events, 3.5 us)
Async XLA Ops:
  0.6 5.7 %copy-start.2 = (f32[4,128,1024]{2,1,0:T(8,128)S(1)}, f32[4,128,1024]{2,1,0:T(8,128)}, u32[]{:S(2)}) copy-start(f32[4,128,1024]{2,1,0:T(8,128)} %param.7) | copy-start | bytes 6291460
  0.7 10.1 %copy-start = (f32[4,128,1024]{2,1,0:T(8,128)S(1)}, f32[4,128,1024]{2,1,0:T(8,128)}, u32[]{:S(2)}) copy-start(f32[4,128,1024]{2,1,0:T(8,128)} %param.8) | copy-start | bytes 6291460
  3.8 15.3 %copy-start.8 = (f32[4,128,1024]{2,1,0:T(8,128)S(1)}, f32[4,128,1024]{2,1,0:T(8,128)}, u32[]{:S(2)}) copy-start(f32[4,128,1024]{2,1,0:T(8,128)} %param.11) | copy-start | bytes 6291460
  3.8 15.3 %collective-permute-start = (f32[1,128,1024]{2,1,0:T(8,128)S(1)}, f32[1,128,1024]{2,1,0:T(8,128)S(1)}, u32[]{:S(2)}, u32[]{:S(2)}) collective-permute-start(f32[1,128,1024]{2,1,0:T(8,128)S(1)} %slice.202), channel_id=1, source_target_pairs={{0,16},{1,17},{2,18},{3,19},{4,20},{5,21},{6,22},{7,23},{8,24},{9,... | collective-permute-start | bytes 1572872 | tf_op jit(solution)/shard_map/ppermute | solution.py:25
  6.4 12.7 %collective-permute-start.1 = (f32[4,1,1024]{2,1,0:T(1,128)S(1)}, f32[4,1,1024]{2,1,0:T(1,128)S(1)}, u32[]{:S(2)}, u32[]{:S(2)}) collective-permute-start(f32[4,1,1024]{2,1,0:T(1,128)S(1)} %slice.173), channel_id=1, source_target_pairs={{0,4},{4,8},{8,12},{1,5},{5,9},{9,13},{2,6},{6,10},{10,14},{3,7},{... | collective-permute-start | bytes 49160 | tf_op jit(solution)/shard_map/ppermute | solution.py:25
  10.9 8.2 %collective-permute-start.2 = (f32[4,128,1]{2,1,0:T(8,128)S(1)}, f32[4,128,1]{2,1,0:T(8,128)S(1)}, u32[]{:S(2)}, u32[]{:S(2)}) collective-permute-start(f32[4,128,1]{2,1,0:T(8,128)S(1)} %slice.175), channel_id=1, source_target_pairs={{0,1},{1,2},{2,3},{4,5},{5,6},{6,7},{8,9},{9,10},{10,11},{12,13},{... | collective-permute-start | bytes 6152 | tf_op jit(solution)/shard_map/ppermute | solution.py:25
  14.4 53.0 %copy-start.6 = (f32[3,128,1024]{2,1,0:T(8,128)}, f32[3,128,1024]{2,1,0:T(8,128)S(1)}, u32[]{:S(2)}) copy-start(f32[3,128,1024]{2,1,0:T(8,128)S(1)} %slice.206) | copy-start | bytes 4718596
  21.3 2.9 %collective-permute-start.3 = (f32[128,1024]{1,0:T(8,128)S(1)}, f32[128,1024]{1,0:T(8,128)S(1)}, u32[]{:S(2)}, u32[]{:S(2)}) collective-permute-start(f32[128,1024]{1,0:T(8,128)S(1)} %fusion.26), channel_id=1, source_target_pairs={{0,16},{1,17},{2,18},{3,19},{4,20},{5,21},{6,22},{7,23},{8,24},{9,... | collective-permute-start | bytes 1572872 | tf_op jit(solution)/shard_map/ppermute | solution.py:25
  25.2 4.9 %copy-start.23 = (f32[128,1024]{1,0:T(8,128)}, f32[128,1024]{1,0:T(8,128)S(1)}, u32[]{:S(2)}) copy-start(f32[128,1024]{1,0:T(8,128)S(1)} %get-tuple-element.31) | copy-start | bytes 1572868
  25.2 4.9 %copy-start.25 = (f32[128,1024]{1,0:T(8,128)}, f32[128,1024]{1,0:T(8,128)S(1)}, u32[]{:S(2)}) copy-start(f32[128,1024]{1,0:T(8,128)S(1)} %get-tuple-element.33) | copy-start | bytes 1572868
  25.2 4.9 %copy-start.27 = (f32[128,1024]{1,0:T(8,128)}, f32[128,1024]{1,0:T(8,128)S(1)}, u32[]{:S(2)}) copy-start(f32[128,1024]{1,0:T(8,128)S(1)} %get-tuple-element.35) | copy-start | bytes 1572868
  25.2 13.3 %copy-start.13 = (f32[128,1024]{1,0:T(8,128)}, f32[128,1024]{1,0:T(8,128)S(1)}, u32[]{:S(2)}) copy-start(f32[128,1024]{1,0:T(8,128)S(1)} %get-tuple-element.30) | copy-start | bytes 1572868
  25.2 13.3 %copy-start.15 = (f32[128,1024]{1,0:T(8,128)}, f32[128,1024]{1,0:T(8,128)S(1)}, u32[]{:S(2)}) copy-start(f32[128,1024]{1,0:T(8,128)S(1)} %get-tuple-element.32) | copy-start | bytes 1572868
  25.2 13.3 %copy-start.17 = (f32[128,1024]{1,0:T(8,128)}, f32[128,1024]{1,0:T(8,128)S(1)}, u32[]{:S(2)}) copy-start(f32[128,1024]{1,0:T(8,128)S(1)} %get-tuple-element.34) | copy-start | bytes 1572868
  25.2 3.8 %collective-permute-start.4 = (f32[128,1024]{1,0:T(8,128)S(1)}, f32[128,1024]{1,0:T(8,128)S(1)}, u32[]{:S(2)}, u32[]{:S(2)}) collective-permute-start(f32[128,1024]{1,0:T(8,128)S(1)} %get-tuple-element.28), channel_id=1, source_target_pairs={{0,16},{1,17},{2,18},{3,19},{4,20},{5,21},{6,22},{7,23},{8,24},{9,... | collective-permute-start | bytes 1572872 | tf_op jit(solution)/shard_map/ppermute | solution.py:25
  30.1 3.8 %collective-permute-start.5 = (f32[128,1024]{1,0:T(8,128)S(1)}, f32[128,1024]{1,0:T(8,128)S(1)}, u32[]{:S(2)}, u32[]{:S(2)}) collective-permute-start(f32[128,1024]{1,0:T(8,128)S(1)} %get-tuple-element.24), channel_id=1, source_target_pairs={{16,0},{17,1},{18,2},{19,3},{20,4},{21,5},{22,6},{23,7},{24,8},{25... | collective-permute-start | bytes 1572872 | tf_op jit(solution)/shard_map/ppermute | solution.py:25
  34.2 33.2 %copy-start.10 = (f32[128,1024]{1,0:T(8,128)}, f32[128,1024]{1,0:T(8,128)S(1)}, u32[]{:S(2)}) copy-start(f32[128,1024]{1,0:T(8,128)S(1)} %multiply_add_fusion.7) | copy-start | bytes 1572868
  34.2 3.6 %collective-permute-start.6 = (f32[1,128,1024]{2,1,0:T(8,128)S(1)}, f32[1,128,1024]{2,1,0:T(8,128)S(1)}, u32[]{:S(2)}, u32[]{:S(2)}) collective-permute-start(f32[1,128,1024]{2,1,0:T(8,128)S(1)} %bitcast.233), channel_id=1, source_target_pairs={{0,16},{1,17},{2,18},{3,19},{4,20},{5,21},{6,22},{7,23},{8,24},{9,... | collective-permute-start | bytes 1572872 | tf_op jit(solution)/shard_map/ppermute | solution.py:16
  39.0 28.4 %copy-start.19 = (f32[128,1024]{1,0:T(8,128)}, f32[128,1024]{1,0:T(8,128)S(1)}, u32[]{:S(2)}) copy-start(f32[128,1024]{1,0:T(8,128)S(1)} %get-tuple-element.22) | copy-start | bytes 1572868
  39.0 28.4 %copy-start.20 = (f32[128,1024]{1,0:T(8,128)}, f32[128,1024]{1,0:T(8,128)S(1)}, u32[]{:S(2)}) copy-start(f32[128,1024]{1,0:T(8,128)S(1)} %get-tuple-element.23) | copy-start | bytes 1572868
  39.0 28.4 %copy-start.29 = (f32[1,128,1024]{2,1,0:T(8,128)}, f32[1,128,1024]{2,1,0:T(8,128)S(1)}, u32[]{:S(2)}) copy-start(f32[1,128,1024]{2,1,0:T(8,128)S(1)} %get-tuple-element.21) | copy-start | bytes 1572868
  39.0 3.8 %collective-permute-start.7 = (f32[1,128,1024]{2,1,0:T(8,128)S(1)}, f32[1,128,1024]{2,1,0:T(8,128)S(1)}, u32[]{:S(2)}, u32[]{:S(2)}) collective-permute-start(f32[1,128,1024]{2,1,0:T(8,128)S(1)} %get-tuple-element.21), channel_id=1, source_target_pairs={{16,0},{17,1},{18,2},{19,3},{20,4},{21,5},{22,6},{23,7},{24,8},{25... | collective-permute-start | bytes 1572872 | tf_op jit(solution)/shard_map/ppermute | solution.py:17
  42.9 24.5 %copy-start.33 = (f32[1,128,1024]{2,1,0:T(8,128)S(1)}, f32[1,128,1024]{2,1,0:T(8,128)}, u32[]{:S(2)}) copy-start(f32[1,128,1024]{2,1,0:T(8,128)} %copy-done.32) | copy-start | bytes 1572868
  42.9 5.1 %collective-permute-start.9 = (f32[6,1,1024]{2,1,0:T(1,128)S(1)}, f32[6,1,1024]{2,1,0:T(1,128)S(1)}, u32[]{:S(2)}, u32[]{:S(2)}) collective-permute-start(f32[6,1,1024]{2,1,0:T(1,128)S(1)} %get-tuple-element.42), channel_id=1, source_target_pairs={{0,4},{4,8},{8,12},{1,5},{5,9},{9,13},{2,6},{6,10},{10,14},{3,7},{... | collective-permute-start | bytes 73736 | tf_op jit(solution)/shard_map/ppermute | solution.py:16
  46.6 5.7 %collective-permute-start.8 = (f32[6,1,1024]{2,1,0:T(1,128)S(1)}, f32[6,1,1024]{2,1,0:T(1,128)S(1)}, u32[]{:S(2)}, u32[]{:S(2)}) collective-permute-start(f32[6,1,1024]{2,1,0:T(1,128)S(1)} %get-tuple-element.43), channel_id=1, source_target_pairs={{4,0},{8,4},{12,8},{5,1},{9,5},{13,9},{6,2},{10,6},{14,10},{7,3},{... | collective-permute-start | bytes 73736 | tf_op jit(solution)/shard_map/ppermute | solution.py:17
  52.5 14.9 %collective-permute-start.10 = (f32[6,130,1]{2,1,0:T(8,128)S(1)}, f32[6,130,1]{2,1,0:T(8,128)S(1)}, u32[]{:S(2)}, u32[]{:S(2)}) collective-permute-start(f32[6,130,1]{2,1,0:T(8,128)S(1)} %get-tuple-element.38), channel_id=1, source_target_pairs={{1,0},{2,1},{3,2},{5,4},{6,5},{7,6},{9,8},{10,9},{11,10},{13,12},{... | collective-permute-start | bytes 9368 | tf_op jit(solution)/shard_map/ppermute | solution.py:17
  53.8 13.6 %collective-permute-start.11 = (f32[6,130,1]{2,1,0:T(8,128)S(1)}, f32[6,130,1]{2,1,0:T(8,128)S(1)}, u32[]{:S(2)}, u32[]{:S(2)}) collective-permute-start(f32[6,130,1]{2,1,0:T(8,128)S(1)} %get-tuple-element.39), channel_id=1, source_target_pairs={{0,1},{1,2},{2,3},{4,5},{5,6},{6,7},{8,9},{9,10},{10,11},{12,13},{... | collective-permute-start | bytes 9368 | tf_op jit(solution)/shard_map/ppermute | solution.py:16
  128.2 40.4 %copy-start.4 = (f32[4,128,1024]{2,1,0:T(8,128)}, f32[4,128,1024]{2,1,0:T(8,128)S(1)}, u32[]{:S(2)}) copy-start(f32[4,128,1024]{2,1,0:T(8,128)S(1)} %multiply_subtract_fusion.1) | copy-start | bytes 6291460
  128.2 3.6 %copy-start.14 = (f32[128,1024]{1,0:T(8,128)S(1)}, f32[128,1024]{1,0:T(8,128)}, u32[]{:S(2)}) copy-start(f32[128,1024]{1,0:T(8,128)} %copy-done.13) | copy-start | bytes 1572868
  128.2 3.6 %copy-start.16 = (f32[128,1024]{1,0:T(8,128)S(1)}, f32[128,1024]{1,0:T(8,128)}, u32[]{:S(2)}) copy-start(f32[128,1024]{1,0:T(8,128)} %copy-done.15) | copy-start | bytes 1572868
  128.2 3.6 %copy-start.18 = (f32[128,1024]{1,0:T(8,128)S(1)}, f32[128,1024]{1,0:T(8,128)}, u32[]{:S(2)}) copy-start(f32[128,1024]{1,0:T(8,128)} %copy-done.17) | copy-start | bytes 1572868
  128.9 2.9 %collective-permute-start.12 = (f32[128,1024]{1,0:T(8,128)S(1)}, f32[128,1024]{1,0:T(8,128)S(1)}, u32[]{:S(2)}, u32[]{:S(2)}) collective-permute-start(f32[128,1024]{1,0:T(8,128)S(1)} %add_multiply_fusion.3), channel_id=1, source_target_pairs={{0,16},{1,17},{2,18},{3,19},{4,20},{5,21},{6,22},{7,23},{8,24},{9,... | collective-permute-start | bytes 1572872 | tf_op jit(solution)/shard_map/ppermute | solution.py:25
  132.9 3.8 %collective-permute-start.13 = (f32[128,1024]{1,0:T(8,128)S(1)}, f32[128,1024]{1,0:T(8,128)S(1)}, u32[]{:S(2)}, u32[]{:S(2)}) collective-permute-start(f32[128,1024]{1,0:T(8,128)S(1)} %get-tuple-element.15), channel_id=1, source_target_pairs={{16,0},{17,1},{18,2},{19,3},{20,4},{21,5},{22,6},{23,7},{24,8},{25... | collective-permute-start | bytes 1572872 | tf_op jit(solution)/shard_map/ppermute | solution.py:25
  137.0 31.6 %copy-start.12 = (f32[128,1024]{1,0:T(8,128)}, f32[128,1024]{1,0:T(8,128)S(1)}, u32[]{:S(2)}) copy-start(f32[128,1024]{1,0:T(8,128)S(1)} %multiply_add_fusion.3) | copy-start | bytes 1572868
  137.0 3.6 %collective-permute-start.14 = (f32[1,128,1024]{2,1,0:T(8,128)S(1)}, f32[1,128,1024]{2,1,0:T(8,128)S(1)}, u32[]{:S(2)}, u32[]{:S(2)}) collective-permute-start(f32[1,128,1024]{2,1,0:T(8,128)S(1)} %bitcast.236), channel_id=1, source_target_pairs={{0,16},{1,17},{2,18},{3,19},{4,20},{5,21},{6,22},{7,23},{8,24},{9,... | collective-permute-start | bytes 1572872 | tf_op jit(solution)/shard_map/ppermute | solution.py:16
  141.4 27.1 %copy-start.21 = (f32[128,1024]{1,0:T(8,128)}, f32[128,1024]{1,0:T(8,128)S(1)}, u32[]{:S(2)}) copy-start(f32[128,1024]{1,0:T(8,128)S(1)} %get-tuple-element.13) | copy-start | bytes 1572868
  141.4 27.1 %copy-start.22 = (f32[128,1024]{1,0:T(8,128)}, f32[128,1024]{1,0:T(8,128)S(1)}, u32[]{:S(2)}) copy-start(f32[128,1024]{1,0:T(8,128)S(1)} %get-tuple-element.14) | copy-start | bytes 1572868
  141.4 27.2 %copy-start.30 = (f32[1,128,1024]{2,1,0:T(8,128)}, f32[1,128,1024]{2,1,0:T(8,128)S(1)}, u32[]{:S(2)}) copy-start(f32[1,128,1024]{2,1,0:T(8,128)S(1)} %get-tuple-element.12) | copy-start | bytes 1572868
  141.4 3.8 %collective-permute-start.15 = (f32[1,128,1024]{2,1,0:T(8,128)S(1)}, f32[1,128,1024]{2,1,0:T(8,128)S(1)}, u32[]{:S(2)}, u32[]{:S(2)}) collective-permute-start(f32[1,128,1024]{2,1,0:T(8,128)S(1)} %get-tuple-element.12), channel_id=1, source_target_pairs={{16,0},{17,1},{18,2},{19,3},{20,4},{21,5},{22,6},{23,7},{24,8},{25... | collective-permute-start | bytes 1572872 | tf_op jit(solution)/shard_map/ppermute | solution.py:17
  142.7 25.9 %copy-start.9 = (f32[4,128,1024]{2,1,0:T(8,128)S(1)}, f32[4,128,1024]{2,1,0:T(8,128)}, u32[]{:S(2)}) copy-start(f32[4,128,1024]{2,1,0:T(8,128)} %param.11) | copy-start | bytes 6291460
  142.8 25.8 %copy-start.7 = (f32[3,128,1024]{2,1,0:T(8,128)S(1)}, f32[3,128,1024]{2,1,0:T(8,128)}, u32[]{:S(2)}) copy-start(f32[3,128,1024]{2,1,0:T(8,128)} %copy-done.6) | copy-start | bytes 4718596
  145.2 23.4 %copy-start.3 = (f32[4,128,1024]{2,1,0:T(8,128)S(1)}, f32[4,128,1024]{2,1,0:T(8,128)}, u32[]{:S(2)}) copy-start(f32[4,128,1024]{2,1,0:T(8,128)} %param.7) | copy-start | bytes 6291460
  145.3 23.3 %copy-start.1 = (f32[4,128,1024]{2,1,0:T(8,128)S(1)}, f32[4,128,1024]{2,1,0:T(8,128)}, u32[]{:S(2)}) copy-start(f32[4,128,1024]{2,1,0:T(8,128)} %param.8) | copy-start | bytes 6291460
  145.3 4.1 %collective-permute-start.17 = (f32[6,1,1024]{2,1,0:T(1,128)S(1)}, f32[6,1,1024]{2,1,0:T(1,128)S(1)}, u32[]{:S(2)}, u32[]{:S(2)}) collective-permute-start(f32[6,1,1024]{2,1,0:T(1,128)S(1)} %get-tuple-element.40), channel_id=1, source_target_pairs={{0,4},{4,8},{8,12},{1,5},{5,9},{9,13},{2,6},{6,10},{10,14},{3,7},{... | collective-permute-start | bytes 73736 | tf_op jit(solution)/shard_map/ppermute | solution.py:16
  147.9 5.7 %collective-permute-start.16 = (f32[6,1,1024]{2,1,0:T(1,128)S(1)}, f32[6,1,1024]{2,1,0:T(1,128)S(1)}, u32[]{:S(2)}, u32[]{:S(2)}) collective-permute-start(f32[6,1,1024]{2,1,0:T(1,128)S(1)} %get-tuple-element.41), channel_id=1, source_target_pairs={{4,0},{8,4},{12,8},{5,1},{9,5},{13,9},{6,2},{10,6},{14,10},{7,3},{... | collective-permute-start | bytes 73736 | tf_op jit(solution)/shard_map/ppermute | solution.py:17
  153.9 14.7 %collective-permute-start.18 = (f32[6,130,1]{2,1,0:T(8,128)S(1)}, f32[6,130,1]{2,1,0:T(8,128)S(1)}, u32[]{:S(2)}, u32[]{:S(2)}) collective-permute-start(f32[6,130,1]{2,1,0:T(8,128)S(1)} %get-tuple-element.36), channel_id=1, source_target_pairs={{1,0},{2,1},{3,2},{5,4},{6,5},{7,6},{9,8},{10,9},{11,10},{13,12},{... | collective-permute-start | bytes 9368 | tf_op jit(solution)/shard_map/ppermute | solution.py:17
  155.2 13.4 %collective-permute-start.19 = (f32[6,130,1]{2,1,0:T(8,128)S(1)}, f32[6,130,1]{2,1,0:T(8,128)S(1)}, u32[]{:S(2)}, u32[]{:S(2)}) collective-permute-start(f32[6,130,1]{2,1,0:T(8,128)S(1)} %get-tuple-element.37), channel_id=1, source_target_pairs={{0,1},{1,2},{2,3},{4,5},{5,6},{6,7},{8,9},{9,10},{10,11},{12,13},{... | collective-permute-start | bytes 9368 | tf_op jit(solution)/shard_map/ppermute | solution.py:16
  168.6 61.5 %copy-start.11 = (f32[128,1024]{1,0:T(8,128)S(1)}, f32[128,1024]{1,0:T(8,128)}, u32[]{:S(2)}) copy-start(f32[128,1024]{1,0:T(8,128)} %copy-done.10) | copy-start | bytes 1572868
  (6 other events, 13.5 us)
where the time goes:
time: 237 us; the launch traced here: 236 us
  blocking collectives  94.5 us (40%)
  waiting for transfers between devices  47.5 us (20%)
  starting transfers between devices  46.2 us (19%)
  other arithmetic  38.5 us (16%)
  between operations  7.43 us (3%)
    psum x2, blocking collectives, paired_sums(): lax.psum((jnp.sum(residual * precond), jnp.sum(image * precond)), ('layer...  94.5 us
    ppermute x6, waiting for transfers between devices, extended(): after = lax.ppermute(initial, axis, down)  30.2 us
    ppermute x6, starting transfers between devices, extended(): before = lax.ppermute(last, axis, up)  20.2 us
    reduce_sum x2, other arithmetic, paired_sums(): jnp.sum(image * precond)  19 us
    ppermute x8, starting transfers between devices, from_behind(): return lax.ppermute(value, axis, pairs)  18.3 us
    ppermute x8, waiting for transfers between devices, from_behind(): return lax.ppermute(value, axis, pairs)  13.9 us
    sub x2, other arithmetic, shards(): residual = residual - alpha * along  8.69 us
    ppermute x6, starting transfers between devices, extended(): after = lax.ppermute(initial, axis, down)  7.74 us
  transfers between devices with their start and end apart: 20, of which 16 were waited for; matrix products, arithmetic and copies ran while one was open for 0% of the time, Pallas kernels for 0%

commit v1 on v0

v1 whole, which is shorter than its diff:
```python
import jax
import jax.numpy as jnp
from jax import lax
from jax.experimental import pallas as pl
from jax.experimental.pallas import tpu as pltpu
from jax.sharding import PartitionSpec as P

GROUPS = 4
SUB = 8
LANE = 128


def kernel(
    r_hbm, rc_hbm, cc_hbm, via_hbm, mask_hbm, gr_hbm,
    x_hbm, res_hbm,
    R, RC, CC, VI, MK, GR, RU, CL, C, INV, ZP, YP, W, V,
    PV, PM, SF1, SG, SF2, PF1, PG, PF2, E,
    stage_row, stage_col, row_send, row_recv, col_send, col_recv, HL0, HL, HR,
    sums_send, sums_py, sums_px, sums_layer,
    load_sem, stage_sem, plane_send_sem, plane_recv_sem, swap_send_sem, swap_recv_sem,
    row_send_sem, row_recv_sem, col_send_sem, col_recv_sem,
    py_send_sem, py_recv_sem, px_send_sem, px_recv_sem, la_send_sem, la_recv_sem, out_sem,
):
    depth, rows, cols = r_hbm.shape
    npx, npy = lax.axis_size("px"), lax.axis_size("py")
    core, px, py = lax.axis_index("layer"), lax.axis_index("px"), lax.axis_index("py")
    other = 1 - core
    size = rows // GROUPS
    chunks = size // SUB

    def remote(src, dst, send_sem, recv_sem, where):
        return pltpu.make_async_remote_copy(
            src_ref=src, dst_ref=dst, send_sem=send_sem, recv_sem=recv_sem,
            device_id=where, device_id_type=pl.DeviceIdType.MESH)

    stage = [
        pltpu.make_async_copy(rc_hbm.at[:, pl.ds(rows - SUB, SUB), :], stage_row, stage_sem.at[0]),
        pltpu.make_async_copy(cc_hbm.at[:, :, pl.ds(cols - LANE, LANE)], stage_col, stage_sem.at[1]),
    ]
    for copy in stage:
        copy.start()
    own_planes = [
        pltpu.make_async_copy(via_hbm.at[depth - 1], PV, plane_recv_sem.at[0]),
        pltpu.make_async_copy(mask_hbm.at[depth - 1], PM, plane_recv_sem.at[1]),
    ]

    @pl.when(core == 0)
    def _():
        for copy in own_planes:
            copy.start()

    loads = []
    for g in range(GROUPS):
        here = pl.ds(g * size, size)
        padded = pl.ds(SUB + g * size, size)
        pairs = ((rc_hbm, RC, padded), (cc_hbm, CC, here), (via_hbm, VI, here),
                 (mask_hbm, MK, here), (gr_hbm, GR, here), (r_hbm, R, here))
        group = [pltpu.make_async_copy(src.at[:, here, :], dst.at[:, at, :], load_sem.at[g, n])
                 for n, (src, dst, at) in enumerate(pairs)]
        for copy in group:
            copy.start()
        loads.append(group)

    barrier = pltpu.get_barrier_semaphore()
    for d in range(1, npy):
        pl.semaphore_signal(barrier, inc=1, device_id={"py": lax.rem(py + d, npy)},
                            device_id_type=pl.DeviceIdType.MESH)
    for d in range(1, npx):
        pl.semaphore_signal(barrier, inc=1, device_id={"px": lax.rem(px + d, npx)},
                            device_id_type=pl.DeviceIdType.MESH)
    pl.semaphore_signal(barrier, inc=1, device_id={"layer": other}, device_id_type=pl.DeviceIdType.MESH)

    @pl.when(px == 0)
    def _():
        for n in range(3):
            row_recv[n, 0] = jnp.zeros((depth, 1, cols), jnp.float32)

    @pl.when(px == npx - 1)
    def _():
        for n in range(3):
            row_recv[n, 1] = jnp.zeros((depth, 1, cols), jnp.float32)

    @pl.when(py == 0)
    def _():
        for n in range(3):
            col_recv[n, 0] = jnp.zeros((SUB, rows), jnp.float32)

    @pl.when(py == npy - 1)
    def _():
        for n in range(3):
            col_recv[n, 1] = jnp.zeros((SUB, rows), jnp.float32)

    pl.semaphore_wait(barrier, npy + npx - 1)

    planes = [
        remote(via_hbm.at[depth - 1], PV, plane_send_sem.at[0], plane_recv_sem.at[0], {"layer": other}),
        remote(mask_hbm.at[depth - 1], PM, plane_send_sem.at[1], plane_recv_sem.at[1], {"layer": other}),
    ]

    @pl.when(core == 0)
    def _():
        for copy in planes:
            copy.start()

    lane = lax.broadcasted_iota(jnp.int32, (SUB, LANE), 1)
    sub = lax.broadcasted_iota(jnp.int32, (SUB, cols), 0)
    lane_tall = lax.broadcasted_iota(jnp.int32, (rows, LANE), 1)

    def row_copy(n, side):
        to = px + 1 if side == 0 else px - 1
        return remote(row_send.at[n, side], row_recv.at[n, side], row_send_sem.at[n, side],
                      row_recv_sem.at[n, side], {"px": to})

    def col_copy(n, side):
        to = py + 1 if side == 0 else py - 1
        return remote(col_send.at[n, side], col_recv.at[n, side], col_send_sem.at[n, side],
                      col_recv_sem.at[n, side], {"py": to})

    def guarded(n, sides, what):
        for side in sides:
            row_out = px < npx - 1 if side == 0 else px > 0
            col_out = py < npy - 1 if side == 0 else py > 0
            row_in = px > 0 if side == 0 else px < npx - 1
            col_in = py > 0 if side == 0 else py < npy - 1
            if what == "start":
                pl.when(col_out)(lambda s=side: col_copy(n, s).start())
                pl.when(row_out)(lambda s=side: row_copy(n, s).start())
            elif what == "recv":
                pl.when(row_in)(lambda s=side: row_copy(n, s).wait_recv())
                pl.when(col_in)(lambda s=side: col_copy(n, s).wait_recv())
            else:
                pl.when(row_out)(lambda s=side: row_copy(n, s).wait_send())
                pl.when(col_out)(lambda s=side: col_copy(n, s).wait_send())

    def pack_columns(tile_of, at):
        packed = jnp.zeros((rows, LANE), jnp.float32)
        for l in range(depth):
            column = jnp.broadcast_to(tile_of(l)[:, at:at + 1], (rows, LANE))
            packed = jnp.where(lane_tall == l, column, packed)
        return jnp.transpose(packed)[:SUB, :]

    def unpack_columns(n, side, dst):
        tall = jnp.transpose(jnp.concatenate(
            [col_recv[n, side], jnp.zeros((LANE - SUB, rows), jnp.float32)], axis=0))
        for l in range(depth):
            dst[l] = jnp.broadcast_to(tall[:, l:l + 1], (rows, LANE))

    def take_rows(n, sides, dst):
        for side in sides:
            at = SUB - 1 if side == 0 else SUB + rows
            for l in range(depth):
                dst[l, pl.ds(at, 1), :] = row_recv[n, side, l]

    for copy in stage:
        copy.wait()
    for l in range(depth):
        row_send[0, 0, l] = stage_row[l, SUB - 1:SUB, :]
    col_send[0, 0] = pack_columns(lambda l: stage_col[l], LANE - 1)
    guarded(0, (0,), "start")

    def shift_left(value, halo):
        rolled = pltpu.roll(value, cols - 1, 1)
        last = jnp.where(lane == LANE - 1, halo, rolled[:, cols - LANE:])
        return jnp.concatenate([rolled[:, :cols - LANE], last], axis=1)

    def shift_right(value, halo):
        rolled = pltpu.roll(value, 1, 1)
        first = jnp.where(lane == 0, halo, rolled[:, :LANE])
        return jnp.concatenate([first, rolled[:, LANE:]], axis=1)

    def from_above(value, before):
        return jnp.where(sub == 0, pltpu.roll(before, 1, 0), pltpu.roll(value, 1, 0))

    def from_below(value, after):
        return jnp.where(sub == SUB - 1, pltpu.roll(after, SUB - 1, 0), pltpu.roll(value, SUB - 1, 0))

    def folded(value):
        total = value[:, :LANE]
        for n in range(1, cols // LANE):
            total = total + value[:, n * LANE:(n + 1) * LANE]
        return total

    order = [k + core * (depth - 1 - 2 * k) for k in range(depth)]
    via_at = [k + core * (depth - 2 - 2 * k) for k in range(depth - 1)]

    def span(i, pad=0):
        return pl.ds(pl.multiple_of(i * SUB + pad, SUB), SUB)

    def swap(n, src, dst, g):
        here = pl.ds(g * size, size)
        return remote(src.at[here, :], dst.at[here, :], swap_send_sem.at[n, g], swap_recv_sem.at[n, g],
                      {"layer": other})

    guarded(0, (0,), "recv")
    take_rows(0, (0,), RC)
    unpack_columns(0, 0, HL0)

    @pl.when(core == 0)
    def _():
        for copy in own_planes:
            copy.wait()

    @pl.when(core == 1)
    def _():
        for copy in planes:
            copy.wait_recv()

    def factor(i, carry):
        here = span(i)
        before_c = before_g = before_f = None
        for k in range(depth):
            l = order[k]
            rc = RC[l, span(i, SUB), :]
            ru = from_above(rc, RC[l, here, :])
            cc = CC[l, here, :]
            cl = shift_right(cc, HL0[l, here, :])
            RU[l, here, :] = ru
            CL[l, here, :] = cl
            if k < depth - 1:
                c = VI[via_at[k], here, :] * MK[via_at[k], here, :].astype(jnp.float32)
            else:
                c = PV[here, :] * PM[here, :].astype(jnp.float32)
            diagonal = GR[l, here, :] + rc + ru + cc + cl + c
            r = R[l, here, :]
            if k:
                diagonal = (diagonal + before_c) - before_c * before_g
                r = r + before_c * before_f
            inverse = 1.0 / diagonal
            f = r * inverse
            g = c * inverse
            C[k, here, :] = c
            INV[l, here, :] = inverse
            ZP[l, span(i, SUB), :] = f
            before_c, before_g, before_f = c, g, f
        SF1[here, :] = before_f
        SG[here, :] = before_g
        return carry

    for g in range(GROUPS):
        for copy in loads[g]:
            copy.wait()
        lax.fori_loop(g * chunks, (g + 1) * chunks, factor, 0)
        swap(0, SF1, PF1, g).start()
        swap(1, SG, PG, g).start()

    def back_first(i, total):
        here = span(i)
        own_g = SG[here, :]
        e = 1.0 / (1.0 - own_g * PG[here, :])
        E[here, :] = e
        value = (SF1[here, :] + own_g * PF1[here, :]) * e
        ZP[order[-1], span(i, SUB), :] = value
        total = total + folded(value * R[order[-1], here, :])
        for k in range(depth - 2, -1, -1):
            l = order[k]
            value = ZP[l, span(i, SUB), :] + C[k, here, :] * INV[l, here, :] * value
            ZP[l, span(i, SUB), :] = value
            total = total + folded(value * R[l, here, :])
        return total

    zero = jnp.zeros((SUB, LANE), jnp.float32)
    b0 = zero
    for g in range(GROUPS):
        swap(0, SF1, PF1, g).wait_recv()
        swap(1, SG, PG, g).wait_recv()
        b0 = lax.fori_loop(g * chunks, (g + 1) * chunks, back_first, b0)

    def send_halos(n, field):
        inner = pl.ds(SUB, rows)
        for l in range(depth):
            row_send[n, 0, l] = field[l, pl.ds(SUB + rows - 1, 1), :]
            row_send[n, 1, l] = field[l, pl.ds(SUB, 1), :]
        col_send[n, 0] = pack_columns(lambda l: field[l, inner, cols - LANE:], LANE - 1)
        col_send[n, 1] = pack_columns(lambda l: field[l, inner, :LANE], 0)
        guarded(n, (0, 1), "start")

    def recv_halos(n, field):
        guarded(n, (0, 1), "recv")
        take_rows(n, (0, 1), field)
        unpack_columns(n, 0, HL)
        unpack_columns(n, 1, HR)

    def lateral(field, l, i):
        here = span(i)
        value = field[l, span(i, SUB), :]
        total = RC[l, span(i, SUB), :] * from_below(value, field[l, span(i, 2 * SUB), :])
        total = total + RU[l, here, :] * from_above(value, field[l, here, :])
        total = total + CC[l, here, :] * shift_left(value, HR[l, here, :])
        total = total + CL[l, here, :] * shift_right(value, HL[l, here, :])
        return value, total

    send_halos(1, ZP)
    recv_halos(1, ZP)

    def image_first(i, total):
        here = span(i)
        before_f = None
        for k in range(depth):
            l = order[k]
            value, around = lateral(ZP, l, i)
            w = R[l, here, :] - around
            W[l, here, :] = w
            total = total + folded(value * w)
            if k:
                w = w + C[k - 1, here, :] * before_f
            before_f = w * INV[l, here, :]
            YP[l, span(i, SUB), :] = before_f
        SF2[here, :] = before_f
        return total

    g00 = zero
    for g in range(GROUPS):
        g00 = lax.fori_loop(g * chunks, (g + 1) * chunks, image_first, g00)
        swap(2, SF2, PF2, g).start()

    def back_second(i, total):
        here = span(i)
        value = (SF2[here, :] + SG[here, :] * PF2[here, :]) * E[here, :]
        YP[order[-1], span(i, SUB), :] = value
        total = total + folded(value * W[order[-1], here, :])
        for k in range(depth - 2, -1, -1):
            l = order[k]
            value = YP[l, span(i, SUB), :] + C[k, here, :] * INV[l, here, :] * value
            YP[l, span(i, SUB), :] = value
            total = total + folded(value * W[l, here, :])
        return total

    g01 = zero
    for g in range(GROUPS):
        swap(2, SF2, PF2, g).wait_recv()
        g01 = lax.fori_loop(g * chunks, (g + 1) * chunks, back_second, g01)

    send_halos(2, YP)
    recv_halos(2, YP)

    def image_second(i, total):
        here = span(i)
        for l in range(depth):
            value, around = lateral(YP, l, i)
            v = W[l, here, :] - around
            V[l, here, :] = v
            total = total + folded(value * v)
        return total

    g11 = lax.fori_loop(0, rows // SUB, image_second, zero)

    parts = [jnp.sum(value, axis=0, keepdims=True) for value in (b0, g00, g01, g11)]
    partial = jnp.concatenate(parts + [jnp.zeros((SUB - 4, LANE), jnp.float32)], axis=0)

    def all_sum(partial, stage_at, axis, me, count, buffer, send_sem, recv_sem):
        sums_send[stage_at] = partial
        buffer[me] = partial

        def copy(d, slot):
            return remote(sums_send.at[stage_at], buffer.at[slot], send_sem.at[d], recv_sem.at[slot],
                          {axis: lax.rem(me + d, count)})

        for d in range(1, count):
            copy(d, me).start()
        for d in range(1, count):
            copy(d, lax.rem(me + count - d, count)).wait_recv()
        for d in range(1, count):
            copy(d, me).wait_send()
        total = buffer[0]
        for n in range(1, count):
            total = total + buffer[n]
        return total

    partial = all_sum(partial, 0, "layer", core, 2, sums_layer, la_send_sem, la_recv_sem)
    partial = all_sum(partial, 1, "py", py, npy, sums_py, py_send_sem, py_recv_sem)
    partial = all_sum(partial, 2, "px", px, npx, sums_px, px_send_sem, px_recv_sem)
    flat = jnp.sum(partial, axis=1, keepdims=True)
    base = flat[1:2, :]
    h0 = flat[0:1, :] / base
    h1 = flat[2:3, :] / base
    h2 = flat[3:4, :] / base
    det = h2 - h1 * h1
    c0 = (h0 * h2 - h1) / det
    c1 = (1.0 - h1 * h0) / det

    def finish(i, carry):
        here = span(i)
        for l in range(depth):
            inner = span(i, SUB)
            YP[l, inner, :] = c0 * ZP[l, inner, :] + c1 * YP[l, inner, :]
            V[l, here, :] = R[l, here, :] - c0 * W[l, here, :] - c1 * V[l, here, :]
        return carry

    outs = []
    for g in range(GROUPS):
        lax.fori_loop(g * chunks, (g + 1) * chunks, finish, 0)
        here = pl.ds(g * size, size)
        pair = [
            pltpu.make_async_copy(YP.at[:, pl.ds(SUB + g * size, size), :], x_hbm.at[:, here, :], out_sem.at[g, 0]),
            pltpu.make_async_copy(V.at[:, here, :], res_hbm.at[:, here, :], out_sem.at[g, 1]),
        ]
        for copy in pair:
            copy.start()
        outs += pair

    @pl.when(core == 0)
    def _():
        for copy in planes:
            copy.wait_send()

    guarded(0, (0,), "send")
    guarded(1, (0, 1), "send")
    guarded(2, (0, 1), "send")
    for g in range(GROUPS):
        swap(0, SF1, PF1, g).wait_send()
        swap(1, SG, PG, g).wait_send()
        swap(2, SF2, PF2, g).wait_send()
    for copy in outs:
        copy.wait()


def shards(right_side, row_conduct, column_conduct, via_conduct, via_mask, ground_conduct):
    depth, rows, cols = right_side.shape
    npx, npy = lax.axis_size("px"), lax.axis_size("py")
    f32 = jnp.float32
    block = pltpu.VMEM((depth, rows, cols), f32)
    plane = pltpu.VMEM((rows, cols), f32)
    dma = pltpu.SemaphoreType.DMA
    scratch = [
        block, pltpu.VMEM((depth, rows + SUB, cols), f32), block, block,
        pltpu.VMEM((depth, rows, cols), jnp.int32), block, block, block, block, block,
        pltpu.VMEM((depth, rows + 2 * SUB, cols), f32), pltpu.VMEM((depth, rows + 2 * SUB, cols), f32),
        block, block,
        plane, pltpu.VMEM((rows, cols), jnp.int32), plane, plane, plane, plane, plane, plane, plane,
        pltpu.VMEM((depth, SUB, cols), f32), pltpu.VMEM((depth, rows, LANE), f32),
        pltpu.VMEM((3, 2, depth, 1, cols), f32), pltpu.VMEM((3, 2, depth, 1, cols), f32),
        pltpu.VMEM((3, 2, SUB, rows), f32), pltpu.VMEM((3, 2, SUB, rows), f32),
        pltpu.VMEM((depth, rows, LANE), f32), pltpu.VMEM((depth, rows, LANE), f32),
        pltpu.VMEM((depth, rows, LANE), f32),
        pltpu.VMEM((3, SUB, LANE), f32), pltpu.VMEM((npy, SUB, LANE), f32),
        pltpu.VMEM((npx, SUB, LANE), f32), pltpu.VMEM((2, SUB, LANE), f32),
        dma((GROUPS, 6)), dma((2,)), dma((2,)), dma((2,)), dma((3, GROUPS)), dma((3, GROUPS)),
        dma((3, 2)), dma((3, 2)), dma((3, 2)), dma((3, 2)),
        dma((npy,)), dma((npy,)), dma((npx,)), dma((npx,)), dma((2,)), dma((2,)), dma((GROUPS, 2)),
    ]
    anywhere = pl.BlockSpec(memory_space=pl.ANY)
    out = jax.ShapeDtypeStruct((depth, rows, cols), f32)
    return pl.pallas_call(
        kernel,
        out_shape=(out, out),
        in_specs=[anywhere] * 6,
        out_specs=(anywhere, anywhere),
        scratch_shapes=scratch,
        compiler_params=pltpu.CompilerParams(
            collective_id=0, has_side_effects=True, vmem_limit_bytes=60 * 1024 * 1024),
        name="pcg",
    )(right_side, row_conduct, column_conduct, via_conduct, via_mask, ground_conduct)


def solution(mesh):
    spec = P("layer", "px", "py")
    return jax.shard_map(shards, mesh=mesh, in_specs=(spec,) * 6, out_specs=(spec, spec), check_vma=False)
```

time: 237 us -> 43.3 us (0.18)
  blocking collectives: 94.5 us -> 0 us
  waiting for transfers between devices: 47.5 us -> 0 us
  starting transfers between devices: 46.2 us -> 0 us
  other arithmetic: 38.5 us -> 0 us
  Pallas kernels: 0 us -> 37.9 us
  between operations: 7.43 us -> 0.65 us
  local copies, waits for them, and re-layouts: 1.99 us -> 4.63 us
    psum x2 -> x0, blocking collectives: 94.5 us -> none  [paired_sums(): lax.psum((jnp.sum(residual * precond), jnp.sum(image * precond)), ('layer...]
    ppermute x20 -> x0, waiting for transfers between devices: 47.5 us -> none  [the longest x6 30.2 us: extended(): after = lax.ppermute(initial, axis, down)]
    ppermute x20 -> x0, starting transfers between devices: 46.2 us -> none  [the longest x6 20.2 us: extended(): before = lax.ppermute(last, axis, up)]
    pallas_call x0 -> x1, Pallas kernels: none -> 37.9 us  [shards(): pl.pallas_call(kernel, out_shape=(out, out), in_specs=[anywhere] * 6, out...]
    reduce_sum x2 -> x0, other arithmetic: 19 us -> none  [paired_sums(): jnp.sum(image * precond)]
    sub x2 -> x0, other arithmetic: 8.69 us -> none  [shards(): residual = residual - alpha * along]
    mul x4 -> x0, other arithmetic: 5.01 us -> none  [the longest x1 3.07 us: shards(): vertical = via_conduct * via_mask.astype(jnp.float32) * keep]
    add x5 -> x0, other arithmetic: 4.41 us -> none  [the longest x4 2.57 us: back_layers(): following = forward[index] + gains[index] * following]
  transfers between devices with their start and end apart: 20 -> 0, of which waited for: 16 -> 0; matrix products, arithmetic and copies ran while one was open for 0% -> 0% of each run, Pallas kernels for 0% -> 0%
where the time goes in v1:
time: 43.3 us; the launch traced here: 43.2 us
  Pallas kernels  37.9 us (88%)
  local copies, waits for them, and re-layouts  4.63 us (11%)
  between operations  0.65 us (2%)
    pallas_call x1, Pallas kernels, shards(): pl.pallas_call(kernel, out_shape=(out, out), in_specs=[anywhere] * 6, out...  37.9 us
    unnamed x4, local copies, waits for them, and re-layouts  4.63 us

profile of v1, /device:TPU:0, one launch (start us, length us, event | category | flops | bytes accessed | tf_op | source)
XLA Modules:
  0.0 43.2 jit_solution(12222685205179664201)
XLA Ops:
  0.6 37.9 %pcg.1 = (f32[4,128,1024]{2,1,0:T(8,128)}, f32[4,128,1024]{2,1,0:T(8,128)}) custom-call(f32[4,128,1024]{2,1,0:T(8,128)} %r_hbm.1, f32[4,128,1024]{2,1,0:T(8,128)} %rc_hbm.1, f32[4,128,1024]{2,1,0:T(8,128)} %cc_hbm.1, f32[4,128,1024]{2,1,0:T(8,128)} %via_hbm.1, s32[4,128,1024]{2,1,0:T(8,128)} %mask_hbm.1, f32[4,128,1024]{2,1,0:T(8,128)} %gr_hbm.1), custom_call_target="tpu_custom_call" | custom-call | tf_op jit(solution)/shard_map/pcg/pallas_call | solution.py:443
  38.5 0.0 copy-start
  38.5 3.3 %copy.10 = f32[4,128,1024]{2,1,0:T(8,128)} copy(f32[4,128,1024]{2,1,0:T(8,128)} %get-tuple-element.4) | data formatting | bytes 4194304
  41.8 0.0 copy-done
  41.8 1.3 %copy.11 = f32[4,128,1024]{2,1,0:T(8,128)} copy(f32[4,128,1024]{2,1,0:T(8,128)S(1)} %copy-done) | data formatting | bytes 4194304
Async XLA Ops:
  38.5 3.3 %copy-start = (f32[4,128,1024]{2,1,0:T(8,128)S(1)}, f32[4,128,1024]{2,1,0:T(8,128)}, u32[]{:S(2)}) copy-start(f32[4,128,1024]{2,1,0:T(8,128)} %get-tuple-element.5) | copy-start | bytes 6291460

commit v2 on v1

--- a/solution.py
+++ b/solution.py
@@ -8,18 +8,19 @@
 GROUPS = 4
 SUB = 8
 LANE = 128
+VMEM_LIMIT = 52 * 1024 * 1024
 
 
 def kernel(
     r_hbm, rc_hbm, cc_hbm, via_hbm, mask_hbm, gr_hbm,
-    x_hbm, res_hbm,
-    R, RC, CC, VI, MK, GR, RU, CL, C, INV, ZP, YP, W, V,
+    ZP, YP, W, V, R, coef_z, coef_y, coef_w, coef_v,
+    RC, CC, VI, MK, GR, RU, CL, C, INV,
     PV, PM, SF1, SG, SF2, PF1, PG, PF2, E,
     stage_row, stage_col, row_send, row_recv, col_send, col_recv, HL0, HL, HR,
-    sums_send, sums_py, sums_px, sums_layer,
+    sums_send, sums_plane, sums_px,
     load_sem, stage_sem, plane_send_sem, plane_recv_sem, swap_send_sem, swap_recv_sem,
     row_send_sem, row_recv_sem, col_send_sem, col_recv_sem,
-    py_send_sem, py_recv_sem, px_send_sem, px_recv_sem, la_send_sem, la_recv_sem, out_sem,
+    plane_sum_send, plane_sum_recv, px_send_sem, px_recv_sem,
 ):
     depth, rows, cols = r_hbm.shape
     npx, npy = lax.axis_size("px"), lax.axis_size("py")
@@ -62,13 +63,19 @@
         loads.append(group)
 
     barrier = pltpu.get_barrier_semaphore()
-    for d in range(1, npy):
-        pl.semaphore_signal(barrier, inc=1, device_id={"py": lax.rem(py + d, npy)},
-                            device_id_type=pl.DeviceIdType.MESH)
-    for d in range(1, npx):
-        pl.semaphore_signal(barrier, inc=1, device_id={"px": lax.rem(px + d, npx)},
-                            device_id_type=pl.DeviceIdType.MESH)
-    pl.semaphore_signal(barrier, inc=1, device_id={"layer": other}, device_id_type=pl.DeviceIdType.MESH)
+    wide = 2 * npy
+    mine = core * npy + py
+
+    def in_plane(d):
+        at = lax.rem(mine + d, wide)
+        return {"layer": at // npy, "py": lax.rem(at, npy)}
+
+    def in_px(d):
+        return {"px": lax.rem(px + d, npx)}
+
+    for peers, count in ((in_plane, wide), (in_px, npx)):
+        for d in range(1, count):
+            pl.semaphore_signal(barrier, inc=1, device_id=peers(d), device_id_type=pl.DeviceIdType.MESH)
 
     @pl.when(px == 0)
     def _():
@@ -90,7 +97,7 @@
         for n in range(3):
             col_recv[n, 1] = jnp.zeros((SUB, rows), jnp.float32)
 
-    pl.semaphore_wait(barrier, npy + npx - 1)
+    pl.semaphore_wait(barrier, wide + npx - 2)
 
     planes = [
         remote(via_hbm.at[depth - 1], PV, plane_send_sem.at[0], plane_recv_sem.at[0], {"layer": other}),
@@ -300,7 +307,7 @@
             value, around = lateral(ZP, l, i)
             w = R[l, here, :] - around
             W[l, here, :] = w
-            total = total + folded(value * w)
+            total = (total[0] + folded(value * w), total[1] + folded(value * around))
             if k:
                 w = w + C[k - 1, here, :] * before_f
             before_f = w * INV[l, here, :]
@@ -308,10 +315,11 @@
         SF2[here, :] = before_f
         return total
 
-    g00 = zero
+    g00 = (zero, zero)
     for g in range(GROUPS):
         g00 = lax.fori_loop(g * chunks, (g + 1) * chunks, image_first, g00)
         swap(2, SF2, PF2, g).start()
+    g00, s1 = g00
 
     def back_second(i, total):
         here = span(i)
@@ -337,23 +345,23 @@
         here = span(i)
         for l in range(depth):
             value, around = lateral(YP, l, i)
-            v = W[l, here, :] - around
-            V[l, here, :] = v
-            total = total + folded(value * v)
-        return total
-
-    g11 = lax.fori_loop(0, rows // SUB, image_second, zero)
-
-    parts = [jnp.sum(value, axis=0, keepdims=True) for value in (b0, g00, g01, g11)]
-    partial = jnp.concatenate(parts + [jnp.zeros((SUB - 4, LANE), jnp.float32)], axis=0)
-
-    def all_sum(partial, stage_at, axis, me, count, buffer, send_sem, recv_sem):
+            V[l, here, :] = around
+            z = ZP[l, span(i, SUB), :]
+            total = (total[0] + folded(value * (W[l, here, :] - around)),
+                     total[1] + folded(z * around), total[2] + folded((z - value) * around))
+        return total
+
+    g11, q01, q11 = lax.fori_loop(0, rows // SUB, image_second, (zero, zero, zero))
+
+    parts = [jnp.sum(value, axis=0, keepdims=True) for value in (b0, g00, g01, g11, s1, q01, q11)]
+    partial = jnp.concatenate(parts + [jnp.zeros((1, LANE), jnp.float32)], axis=0)
+
+    def all_sum(partial, stage_at, peers, me, count, buffer, send_sem, recv_sem):
         sums_send[stage_at] = partial
         buffer[me] = partial
 
         def copy(d, slot):
-            return remote(sums_send.at[stage_at], buffer.at[slot], send_sem.at[d], recv_sem.at[slot],
-                          {axis: lax.rem(me + d, count)})
+            return remote(sums_send.at[stage_at], buffer.at[slot], send_sem.at[d], recv_sem.at[slot], peers(d))
 
         for d in range(1, count):
             copy(d, me).start()
@@ -366,37 +374,27 @@
             total = total + buffer[n]
         return total
 
-    partial = all_sum(partial, 0, "layer", core, 2, sums_layer, la_send_sem, la_recv_sem)
-    partial = all_sum(partial, 1, "py", py, npy, sums_py, py_send_sem, py_recv_sem)
-    partial = all_sum(partial, 2, "px", px, npx, sums_px, px_send_sem, px_recv_sem)
-    flat = jnp.sum(partial, axis=1, keepdims=True)
-    base = flat[1:2, :]
-    h0 = flat[0:1, :] / base
-    h1 = flat[2:3, :] / base
-    h2 = flat[3:4, :] / base
-    det = h2 - h1 * h1
-    c0 = (h0 * h2 - h1) / det
-    c1 = (1.0 - h1 * h0) / det
-
-    def finish(i, carry):
-        here = span(i)
-        for l in range(depth):
-            inner = span(i, SUB)
-            YP[l, inner, :] = c0 * ZP[l, inner, :] + c1 * YP[l, inner, :]
-            V[l, here, :] = R[l, here, :] - c0 * W[l, here, :] - c1 * V[l, here, :]
-        return carry
-
-    outs = []
-    for g in range(GROUPS):
-        lax.fori_loop(g * chunks, (g + 1) * chunks, finish, 0)
-        here = pl.ds(g * size, size)
-        pair = [
-            pltpu.make_async_copy(YP.at[:, pl.ds(SUB + g * size, size), :], x_hbm.at[:, here, :], out_sem.at[g, 0]),
-            pltpu.make_async_copy(V.at[:, here, :], res_hbm.at[:, here, :], out_sem.at[g, 1]),
-        ]
-        for copy in pair:
-            copy.start()
-        outs += pair
+    partial = all_sum(partial, 0, in_plane, mine, wide, sums_plane, plane_sum_send, plane_sum_recv)
+    partial = all_sum(partial, 1, in_px, px, npx, sums_px, px_send_sem, px_recv_sem)
+    flat = jnp.broadcast_to(jnp.sum(partial, axis=1, keepdims=True), (SUB, LANE))
+    b0, g00, g01, g11, s1, q01, q11 = (flat[n:n + 1, :] / flat[1:2, :] for n in range(7))
+    det_q = q11 - q01 * q01
+    a_q = (b0 * q11 - q01 * s1) / det_q
+    b_q = (s1 - q01 * b0) / det_q
+    det_y = g11 - g01 * g01
+    c1 = (1.0 - g01 * b0) / det_y
+    c0 = (b0 * g11 - g01) / det_y
+    take_q = q01 * q01 * g11 <= g01 * g01 * q11
+    a = jnp.where(take_q, a_q, c0 + c1)
+    b = jnp.where(take_q, b_q, -c1)
+
+    def spread(value):
+        return jnp.concatenate([value] * (cols // LANE), axis=1)
+
+    coef_z[...] = spread(a + b)
+    coef_y[...] = spread(-b)
+    coef_w[...] = spread(a)
+    coef_v[...] = spread(b)
 
     @pl.when(core == 0)
     def _():
@@ -410,8 +408,6 @@
         swap(0, SF1, PF1, g).wait_send()
         swap(1, SG, PG, g).wait_send()
         swap(2, SF2, PF2, g).wait_send()
-    for copy in outs:
-        copy.wait()
 
 
 def shards(right_side, row_conduct, column_conduct, via_conduct, via_mask, ground_conduct):
@@ -422,34 +418,36 @@
     plane = pltpu.VMEM((rows, cols), f32)
     dma = pltpu.SemaphoreType.DMA
     scratch = [
-        block, pltpu.VMEM((depth, rows + SUB, cols), f32), block, block,
+        pltpu.VMEM((depth, rows + SUB, cols), f32), block, block,
         pltpu.VMEM((depth, rows, cols), jnp.int32), block, block, block, block, block,
-        pltpu.VMEM((depth, rows + 2 * SUB, cols), f32), pltpu.VMEM((depth, rows + 2 * SUB, cols), f32),
-        block, block,
         plane, pltpu.VMEM((rows, cols), jnp.int32), plane, plane, plane, plane, plane, plane, plane,
         pltpu.VMEM((depth, SUB, cols), f32), pltpu.VMEM((depth, rows, LANE), f32),
         pltpu.VMEM((3, 2, depth, 1, cols), f32), pltpu.VMEM((3, 2, depth, 1, cols), f32),
         pltpu.VMEM((3, 2, SUB, rows), f32), pltpu.VMEM((3, 2, SUB, rows), f32),
         pltpu.VMEM((depth, rows, LANE), f32), pltpu.VMEM((depth, rows, LANE), f32),
         pltpu.VMEM((depth, rows, LANE), f32),
-        pltpu.VMEM((3, SUB, LANE), f32), pltpu.VMEM((npy, SUB, LANE), f32),
-        pltpu.VMEM((npx, SUB, LANE), f32), pltpu.VMEM((2, SUB, LANE), f32),
+        pltpu.VMEM((2, SUB, LANE), f32), pltpu.VMEM((2 * npy, SUB, LANE), f32),
+        pltpu.VMEM((npx, SUB, LANE), f32),
         dma((GROUPS, 6)), dma((2,)), dma((2,)), dma((2,)), dma((3, GROUPS)), dma((3, GROUPS)),
         dma((3, 2)), dma((3, 2)), dma((3, 2)), dma((3, 2)),
-        dma((npy,)), dma((npy,)), dma((npx,)), dma((npx,)), dma((2,)), dma((2,)), dma((GROUPS, 2)),
+        dma((2 * npy,)), dma((2 * npy,)), dma((npx,)), dma((npx,)),
     ]
     anywhere = pl.BlockSpec(memory_space=pl.ANY)
-    out = jax.ShapeDtypeStruct((depth, rows, cols), f32)
-    return pl.pallas_call(
+    padded = pltpu.VMEM((depth, rows + 2 * SUB, cols), f32)
+    near = pl.BlockSpec(memory_space=pltpu.VMEM)
+    row = pltpu.VMEM((1, cols), f32)
+    z, y, w, v, r, coef_z, coef_y, coef_w, coef_v = pl.pallas_call(
         kernel,
-        out_shape=(out, out),
+        out_shape=(padded, padded, block, block, block, row, row, row, row),
         in_specs=[anywhere] * 6,
-        out_specs=(anywhere, anywhere),
+        out_specs=(near,) * 9,
         scratch_shapes=scratch,
         compiler_params=pltpu.CompilerParams(
-            collective_id=0, has_side_effects=True, vmem_limit_bytes=60 * 1024 * 1024),
+            collective_id=0, has_side_effects=True, vmem_limit_bytes=VMEM_LIMIT),
         name="pcg",
     )(right_side, row_conduct, column_conduct, via_conduct, via_mask, ground_conduct)
+    inner = slice(SUB, SUB + rows)
+    return coef_z * z[:, inner, :] + coef_y * y[:, inner, :], r - coef_w * w - coef_v * v
 
 
 def solution(mesh):

time: 43.3 us -> 39.6 us (0.915)
  local copies, waits for them, and re-layouts: 4.63 us -> 0 us
  other arithmetic: 0 us -> 3.77 us
  Pallas kernels: 37.9 us -> 35.1 us
    unnamed x4 -> x0, local copies, waits for them, and re-layouts: 4.63 us -> none
    sub x0 -> x1, other arithmetic: none -> 3.77 us  [shards(): r - coef_w * w - coef_v * v]
    pallas_call x1, Pallas kernels: 37.9 us -> 35.1 us  [shards(): pl.pallas_call(kernel, out_shape=(padded, padded, block, block, block, ro...]
where the time goes in v2:
time: 39.6 us; the launch traced here: 39.5 us
  Pallas kernels  35.1 us (89%)
  other arithmetic  3.77 us (10%)
  between operations  0.64 us (2%)
    pallas_call x1, Pallas kernels, shards(): pl.pallas_call(kernel, out_shape=(padded, padded, block, block, block, ro...  35.1 us
    sub x1, other arithmetic, shards(): r - coef_w * w - coef_v * v  3.77 us

profile of v2, /device:TPU:0, one launch (start us, length us, event | category | flops | bytes accessed | tf_op | source)
XLA Modules:
  0.0 39.5 jit_solution(8391036325111913295)
XLA Ops:
  0.6 35.1 %pcg.1 = (f32[4,144,1024]{2,1,0:T(8,128)S(1)}, f32[4,144,1024]{2,1,0:T(8,128)S(1)}, f32[4,128,1024]{2,1,0:T(8,128)S(1)}, f32[4,128,1024]{2,1,0:T(8,128)S(1)}, f3...) custom-call(f32[4,128,1024]{2,1,0:T(8,128)} %r_hbm.1, ...), custom_call_target="tpu_custom_call" | custom-call | tf_op jit(solution)/shard_map/pcg/pallas_call | solution.py:439
  35.7 3.8 %multiply_subtract_fusion = (f32[4,128,1024]{2,1,0:T(8,128)}, f32[4,128,1024]{2,1,0:T(8,128)}) fusion(f32[4,128,1024]{2,1,0:T(8,128)S(1)} %get-tuple-element.19, f32[4,128,1024]{2,1,0:T(8,128)S(1)} %get-tuple-element.15, f32[4,128,1024]{2,1,0:T(8,128)S(1)} %get-tuple-element.17, f32[1024]{0:T(1024)S(1)} %bitcast.7, f32[1024]{0:T(1024)S(1)} %bitcast.6, ...), kind=kLoop, calls=%fused_computation | loop fusion | flops 3670016 | bytes 14696448 | tf_op jit(solution)/shard_map/sub | solution.py:450

commit v3 on v2

--- a/solution.py
+++ b/solution.py
@@ -16,7 +16,7 @@
     ZP, YP, W, V, R, coef_z, coef_y, coef_w, coef_v,
     RC, CC, VI, MK, GR, RU, CL, C, INV,
     PV, PM, SF1, SG, SF2, PF1, PG, PF2, E,
-    stage_row, stage_col, row_send, row_recv, col_send, col_recv, HL0, HL, HR,
+    stage_row, stage_col, row_send, row_recv, col_send, col_recv, HL0,
     sums_send, sums_plane, sums_px,
     load_sem, stage_sem, plane_send_sem, plane_recv_sem, swap_send_sem, swap_recv_sem,
     row_send_sem, row_recv_sem, col_send_sem, col_recv_sem,
@@ -76,6 +76,10 @@
     for peers, count in ((in_plane, wide), (in_px, npx)):
         for d in range(1, count):
             pl.semaphore_signal(barrier, inc=1, device_id=peers(d), device_id_type=pl.DeviceIdType.MESH)
+
+    for field in (ZP, YP):
+        field[:, pl.ds(0, SUB), :] = jnp.zeros((depth, SUB, cols), jnp.float32)
+        field[:, pl.ds(SUB + rows, SUB), :] = jnp.zeros((depth, SUB, cols), jnp.float32)
 
     @pl.when(px == 0)
     def _():
@@ -146,17 +150,9 @@
             packed = jnp.where(lane_tall == l, column, packed)
         return jnp.transpose(packed)[:SUB, :]
 
-    def unpack_columns(n, side, dst):
-        tall = jnp.transpose(jnp.concatenate(
+    def unpacked(n, side):
+        return jnp.transpose(jnp.concatenate(
             [col_recv[n, side], jnp.zeros((LANE - SUB, rows), jnp.float32)], axis=0))
-        for l in range(depth):
-            dst[l] = jnp.broadcast_to(tall[:, l:l + 1], (rows, LANE))
-
-    def take_rows(n, sides, dst):
-        for side in sides:
-            at = SUB - 1 if side == 0 else SUB + rows
-            for l in range(depth):
-                dst[l, pl.ds(at, 1), :] = row_recv[n, side, l]
 
     for copy in stage:
         copy.wait()
@@ -199,8 +195,10 @@
                       {"layer": other})
 
     guarded(0, (0,), "recv")
-    take_rows(0, (0,), RC)
-    unpack_columns(0, 0, HL0)
+    tall = unpacked(0, 0)
+    for l in range(depth):
+        RC[l, pl.ds(SUB - 1, 1), :] = row_recv[0, 0, l]
+        HL0[l] = jnp.broadcast_to(tall[:, l:l + 1], (rows, LANE))
 
     @pl.when(core == 0)
     def _():
@@ -281,33 +279,52 @@
         col_send[n, 1] = pack_columns(lambda l: field[l, inner, :LANE], 0)
         guarded(n, (0, 1), "start")
 
-    def recv_halos(n, field):
-        guarded(n, (0, 1), "recv")
-        take_rows(n, (0, 1), field)
-        unpack_columns(n, 0, HL)
-        unpack_columns(n, 1, HR)
-
     def lateral(field, l, i):
         here = span(i)
         value = field[l, span(i, SUB), :]
         total = RC[l, span(i, SUB), :] * from_below(value, field[l, span(i, 2 * SUB), :])
         total = total + RU[l, here, :] * from_above(value, field[l, here, :])
-        total = total + CC[l, here, :] * shift_left(value, HR[l, here, :])
-        total = total + CL[l, here, :] * shift_right(value, HL[l, here, :])
+        total = total + CC[l, here, :] * shift_left(value, 0.0)
+        total = total + CL[l, here, :] * shift_right(value, 0.0)
         return value, total
 
-    send_halos(1, ZP)
-    recv_halos(1, ZP)
+    def apply_halos(n, target, sign, weights):
+        guarded(n, (0, 1), "recv")
+        tall = [unpacked(n, side) for side in range(2)]
+        sums = [jnp.zeros((1, LANE), jnp.float32)] * len(weights)
+        for l in range(depth):
+            for side in range(2):
+                at = 0 if side == 0 else rows - 1
+                coupling = RU[l, pl.ds(0, 1), :] if side == 0 else RC[l, pl.ds(SUB + rows - 1, 1), :]
+                term = coupling * row_recv[n, side, l]
+                target[l, pl.ds(at, 1), :] = target[l, pl.ds(at, 1), :] + sign * term
+                sums = [total + folded(term * weight(l, pl.ds(SUB + at, 1), pl.ds(0, cols)))
+                        for total, weight in zip(sums, weights)]
+            for side in range(2):
+                block = pl.ds(0, LANE) if side == 0 else pl.ds(cols - LANE, LANE)
+                coupling = CL[l, :, block] if side == 0 else CC[l, :, block]
+                edge = lane_tall == (0 if side == 0 else LANE - 1)
+                halo = jnp.broadcast_to(tall[side][:, l:l + 1], (rows, LANE))
+                term = jnp.where(edge, coupling * halo, 0.0)
+                target[l, :, block] = target[l, :, block] + sign * term
+                sums = [total + jnp.sum(term * weight(l, pl.ds(SUB, rows), block), axis=0, keepdims=True)
+                        for total, weight in zip(sums, weights)]
+        return sums
 
     def image_first(i, total):
+        for l in range(depth):
+            value, around = lateral(ZP, l, i)
+            W[l, span(i), :] = R[l, span(i), :] - around
+            total = total + folded(value * around)
+        return total
+
+    def forward_second(i, total):
         here = span(i)
         before_f = None
         for k in range(depth):
             l = order[k]
-            value, around = lateral(ZP, l, i)
-            w = R[l, here, :] - around
-            W[l, here, :] = w
-            total = (total[0] + folded(value * w), total[1] + folded(value * around))
+            w = W[l, here, :]
+            total = total + folded(ZP[l, span(i, SUB), :] * w)
             if k:
                 w = w + C[k - 1, here, :] * before_f
             before_f = w * INV[l, here, :]
@@ -315,11 +332,14 @@
         SF2[here, :] = before_f
         return total
 
-    g00 = (zero, zero)
-    for g in range(GROUPS):
-        g00 = lax.fori_loop(g * chunks, (g + 1) * chunks, image_first, g00)
+    send_halos(1, ZP)
+    s1 = lax.fori_loop(0, rows // SUB, image_first, zero)
+    s1_edge, = apply_halos(1, W, -1.0, (lambda l, i, j: ZP[l, i, j],))
+
+    g00 = zero
+    for g in range(GROUPS):
+        g00 = lax.fori_loop(g * chunks, (g + 1) * chunks, forward_second, g00)
         swap(2, SF2, PF2, g).start()
-    g00, s1 = g00
 
     def back_second(i, total):
         here = span(i)
@@ -339,7 +359,6 @@
         g01 = lax.fori_loop(g * chunks, (g + 1) * chunks, back_second, g01)
 
     send_halos(2, YP)
-    recv_halos(2, YP)
 
     def image_second(i, total):
         here = span(i)
@@ -353,7 +372,14 @@
 
     g11, q01, q11 = lax.fori_loop(0, rows // SUB, image_second, (zero, zero, zero))
 
+    yy_edge, q01_edge, q11_edge = apply_halos(2, V, 1.0, (
+        lambda l, i, j: YP[l, i, j],
+        lambda l, i, j: ZP[l, i, j],
+        lambda l, i, j: ZP[l, i, j] - YP[l, i, j]))
+
     parts = [jnp.sum(value, axis=0, keepdims=True) for value in (b0, g00, g01, g11, s1, q01, q11)]
+    for n, edge in ((3, -yy_edge), (4, s1_edge), (5, q01_edge), (6, q11_edge)):
+        parts[n] = parts[n] + edge
     partial = jnp.concatenate(parts + [jnp.zeros((1, LANE), jnp.float32)], axis=0)
 
     def all_sum(partial, stage_at, peers, me, count, buffer, send_sem, recv_sem):
@@ -424,7 +450,6 @@
         pltpu.VMEM((depth, SUB, cols), f32), pltpu.VMEM((depth, rows, LANE), f32),
         pltpu.VMEM((3, 2, depth, 1, cols), f32), pltpu.VMEM((3, 2, depth, 1, cols), f32),
         pltpu.VMEM((3, 2, SUB, rows), f32), pltpu.VMEM((3, 2, SUB, rows), f32),
-        pltpu.VMEM((depth, rows, LANE), f32), pltpu.VMEM((depth, rows, LANE), f32),
         pltpu.VMEM((depth, rows, LANE), f32),
         pltpu.VMEM((2, SUB, LANE), f32), pltpu.VMEM((2 * npy, SUB, LANE), f32),
         pltpu.VMEM((npx, SUB, LANE), f32),

time: 39.6 us -> 35.9 us (0.907)
  Pallas kernels: 35.1 us -> 31.4 us
    pallas_call x1, Pallas kernels: 35.1 us -> 31.4 us  [shards(): pl.pallas_call(kernel, out_shape=(padded, padded, block, block, block, ro...]
where the time goes in v3:
time: 35.9 us; the launch traced here: 35.8 us
  Pallas kernels  31.4 us (87%)
  other arithmetic  3.77 us (11%)
  between operations  0.64 us (2%)
    pallas_call x1, Pallas kernels, shards(): pl.pallas_call(kernel, out_shape=(padded, padded, block, block, block, ro...  31.4 us
    sub x1, other arithmetic, shards(): r - coef_w * w - coef_v * v  3.77 us

profile of v3, /device:TPU:0, one launch (start us, length us, event | category | flops | bytes accessed | tf_op | source)
XLA Modules:
  0.0 35.8 jit_solution(17834227371485277811)
XLA Ops:
  0.6 31.4 %pcg.1 = (f32[4,144,1024]{2,1,0:T(8,128)S(1)}, f32[4,144,1024]{2,1,0:T(8,128)S(1)}, f32[4,128,1024]{2,1,0:T(8,128)S(1)}, f32[4,128,1024]{2,1,0:T(8,128)S(1)}, f3...) custom-call(f32[4,128,1024]{2,1,0:T(8,128)} %r_hbm.1, ...), custom_call_target="tpu_custom_call" | custom-call | tf_op jit(solution)/shard_map/pcg/pallas_call | solution.py:464
  32.0 3.8 %multiply_subtract_fusion = (f32[4,128,1024]{2,1,0:T(8,128)}, f32[4,128,1024]{2,1,0:T(8,128)}) fusion(f32[4,128,1024]{2,1,0:T(8,128)S(1)} %get-tuple-element.19, f32[4,128,1024]{2,1,0:T(8,128)S(1)} %get-tuple-element.15, f32[4,128,1024]{2,1,0:T(8,128)S(1)} %get-tuple-element.17, f32[1024]{0:T(1024)S(1)} %bitcast.7, f32[1024]{0:T(1024)S(1)} %bitcast.6, ...), kind=kLoop, calls=%fused_computation | loop fusion | flops 3670016 | bytes 14696448 | tf_op jit(solution)/shard_map/sub | solution.py:475

commit v4 on v3

--- a/solution.py
+++ b/solution.py
@@ -5,7 +5,7 @@
 from jax.experimental.pallas import tpu as pltpu
 from jax.sharding import PartitionSpec as P
 
-GROUPS = 4
+GROUPS = 8
 SUB = 8
 LANE = 128
 VMEM_LIMIT = 52 * 1024 * 1024
@@ -56,7 +56,7 @@
         padded = pl.ds(SUB + g * size, size)
         pairs = ((rc_hbm, RC, padded), (cc_hbm, CC, here), (via_hbm, VI, here),
                  (mask_hbm, MK, here), (gr_hbm, GR, here), (r_hbm, R, here))
-        group = [pltpu.make_async_copy(src.at[:, here, :], dst.at[:, at, :], load_sem.at[g, n])
+        group = [pltpu.make_async_copy(src.at[pl.ds(0, dst.shape[0]), here, :], dst.at[:, at, :], load_sem.at[g, n])
                  for n, (src, dst, at) in enumerate(pairs)]
         for copy in group:
             copy.start()
@@ -104,12 +104,14 @@
     pl.semaphore_wait(barrier, wide + npx - 2)
 
     planes = [
-        remote(via_hbm.at[depth - 1], PV, plane_send_sem.at[0], plane_recv_sem.at[0], {"layer": other}),
-        remote(mask_hbm.at[depth - 1], PM, plane_send_sem.at[1], plane_recv_sem.at[1], {"layer": other}),
+        remote(PV, PV, plane_send_sem.at[0], plane_recv_sem.at[0], {"layer": other}),
+        remote(PM, PM, plane_send_sem.at[1], plane_recv_sem.at[1], {"layer": other}),
     ]
 
     @pl.when(core == 0)
     def _():
+        for copy in own_planes:
+            copy.wait()
         for copy in planes:
             copy.start()
 
@@ -199,11 +201,6 @@
     for l in range(depth):
         RC[l, pl.ds(SUB - 1, 1), :] = row_recv[0, 0, l]
         HL0[l] = jnp.broadcast_to(tall[:, l:l + 1], (rows, LANE))
-
-    @pl.when(core == 0)
-    def _():
-        for copy in own_planes:
-            copy.wait()
 
     @pl.when(core == 1)
     def _():
@@ -444,8 +441,8 @@
     plane = pltpu.VMEM((rows, cols), f32)
     dma = pltpu.SemaphoreType.DMA
     scratch = [
-        pltpu.VMEM((depth, rows + SUB, cols), f32), block, block,
-        pltpu.VMEM((depth, rows, cols), jnp.int32), block, block, block, block, block,
+        pltpu.VMEM((depth, rows + SUB, cols), f32), block, pltpu.VMEM((depth - 1, rows, cols), f32),
+        pltpu.VMEM((depth - 1, rows, cols), jnp.int32), block, block, block, block, block,
         plane, pltpu.VMEM((rows, cols), jnp.int32), plane, plane, plane, plane, plane, plane, plane,
         pltpu.VMEM((depth, SUB, cols), f32), pltpu.VMEM((depth, rows, LANE), f32),
         pltpu.VMEM((3, 2, depth, 1, cols), f32), pltpu.VMEM((3, 2, depth, 1, cols), f32),

time: 35.9 us -> 36 us (level)
  no operation moved by 1% of the time
where the time goes in v4:
time: 36 us; the launch traced here: 35.8 us
  Pallas kernels  31.4 us (87%)
  other arithmetic  3.77 us (10%)
  between operations  0.64 us (2%)
    pallas_call x1, Pallas kernels, shards(): pl.pallas_call(kernel, out_shape=(padded, padded, block, block, block, ro...  31.4 us
    sub x1, other arithmetic, shards(): r - coef_w * w - coef_v * v  3.77 us

profile of v4, /device:TPU:0, one launch (start us, length us, event | category | flops | bytes accessed | tf_op | source)
XLA Modules:
  0.0 35.8 jit_solution(1106637038356058428)
XLA Ops:
  0.6 31.4 %pcg.1 = (f32[4,144,1024]{2,1,0:T(8,128)S(1)}, f32[4,144,1024]{2,1,0:T(8,128)S(1)}, f32[4,128,1024]{2,1,0:T(8,128)S(1)}, f32[4,128,1024]{2,1,0:T(8,128)S(1)}, f3...) custom-call(f32[4,128,1024]{2,1,0:T(8,128)} %r_hbm.1, ...), custom_call_target="tpu_custom_call" | custom-call | tf_op jit(solution)/shard_map/pcg/pallas_call | solution.py:461
  32.1 3.8 %multiply_subtract_fusion = (f32[4,128,1024]{2,1,0:T(8,128)}, f32[4,128,1024]{2,1,0:T(8,128)}) fusion(f32[4,128,1024]{2,1,0:T(8,128)S(1)} %get-tuple-element.19, f32[4,128,1024]{2,1,0:T(8,128)S(1)} %get-tuple-element.15, f32[4,128,1024]{2,1,0:T(8,128)S(1)} %get-tuple-element.17, f32[1024]{0:T(1024)S(1)} %bitcast.7, f32[1024]{0:T(1024)S(1)} %bitcast.6, ...), kind=kLoop, calls=%fused_computation | loop fusion | flops 3670016 | bytes 14696448 | tf_op jit(solution)/shard_map/sub | solution.py:472
